TPU v7x, 32 devices: a whole 2x2x4 slice. The times are simulated.
32 devices in a mesh: expert: 2 (over y), dp: 4 (over x, core), shard: 4 (over z).
Axes of the slice: x: 2, y: 2, z: 4, core: 2. Of those that a mesh axis runs over, the one named last changes fastest.
Arguments:
- grad_partials: bfloat16 [4, 2, 4096, 1536], P('dp', 'expert', 'shard'), may hold values from -120 to 120
- momentum: float32 [2, 4, 1024, 1536], P('expert', 'shard', 'dp'), may hold values from -3 to 3
- q_factor: float32 [1536, 2, 384], P(('dp', 'shard'), 'expert'), may hold values from -0.15625 to 0.15625
Outputs:
- next_momentum: float32 [2, 4, 1024, 1536], P('expert', 'shard', 'dp')
- next_factor: float32 [1536, 2, 384], P(('dp', 'shard'), 'expert')
- weight_update: bfloat16 [2, 4096, 1536], P('expert', 'shard')
All inputs are finite; a program needn't handle non-finite values.
Results may differ from a plain program's by a relative error of at most 0.015.
Values may be sent and summed in bfloat16 or wider, within the bound.
A program may use at most 64 MiB of HBM per device.

v0:
```python
import math

import jax
import jax.numpy as jnp
from jax import lax
from jax.sharding import PartitionSpec as P

clip_rms = 0.5
keep_share = 0.95
highest = lax.Precision.HIGHEST


def orthonormal(projected):
    gram_matrix = lax.psum(
        jnp.einsum("emr,ems->ers", projected, projected, precision=highest), ("dp", "shard")
    )
    triangles = jnp.linalg.cholesky(gram_matrix)

    def solve_one(triangle, columns):
        return jax.scipy.linalg.solve_triangular(triangle, columns.T, lower=True).T

    return jax.vmap(solve_one)(triangles, projected)


def shards(grad_partials, momentum, q_factor):
    partial_value = grad_partials[0]
    gradient = lax.psum_scatter(partial_value, "dp", scatter_dimension=1, tiled=True).astype(
        jnp.float32
    )
    momentum_rows = momentum[:, 0]
    experts, local_rows, hidden_width = gradient.shape
    factor_count, _, rank_width = q_factor.shape
    total_rows = local_rows * lax.axis_size("dp") * lax.axis_size("shard")
    entries = float(experts * lax.axis_size("expert") * total_rows * hidden_width)
    square_sum = lax.psum(jnp.sum(gradient * gradient), ("expert", "dp", "shard"))
    clip_scale = clip_rms / jnp.sqrt(square_sum / entries + 1e-06)
    buffer = momentum_rows + clip_scale * gradient
    zeros_init = jnp.zeros((experts, local_rows, rank_width), jnp.float32)
    projected = zeros_init + jnp.einsum(
        "emf,fer->emr",
        buffer,
        lax.all_gather(q_factor.astype(jnp.bfloat16), ("dp", "shard"), axis=0, tiled=True).astype(
            jnp.float32
        ),
        precision=highest,
    )
    ortho_basis = orthonormal(projected)
    right_term = jnp.einsum("emf,emr->fer", buffer, ortho_basis, precision=highest)
    right_factor = lax.psum(right_term, ("dp", "shard"))
    inverse = lax.rsqrt(jnp.sum(right_factor * right_factor, axis=0) + 1e-06)
    offset = (
        lax.axis_index("dp") * lax.axis_size("shard") + lax.axis_index("shard")
    ) * factor_count
    next_factor = lax.dynamic_slice_in_dim(right_factor, offset, factor_count, 0) * inverse[None]
    correction = jnp.einsum("emr,fer->emf", ortho_basis, right_factor, precision=highest)
    direction = jnp.einsum(
        "emr,fer->emf", ortho_basis * inverse[:, None, :], right_factor, precision=highest
    )
    next_momentum = (buffer - (1.0 - keep_share) * correction)[:, None]
    unit_scale = math.sqrt(total_rows * hidden_width / rank_width)
    local_update = (unit_scale * direction).astype(jnp.bfloat16)
    weight_update = lax.all_gather(local_update, "dp", axis=1, tiled=True)
    return (next_momentum, next_factor, weight_update)


def solution(mesh):
    placed = (
        P("dp", "expert", "shard", None),
        P("expert", "shard", "dp", None),
        P(("dp", "shard"), "expert", None),
    )
    return jax.shard_map(
        shards,
        mesh=mesh,
        in_specs=placed,
        out_specs=(
            P("expert", "shard", "dp", None),
            P(("dp", "shard"), "expert", None),
            P("expert", "shard", None),
        ),
        check_vma=False,
    )
```

profile of v0, /device:TPU:0, one launch (start us, length us, event | category | flops | bytes accessed | tf_op | source)
XLA Modules:
  0.0 446.0 jit_solution(1453472707407732005)
XLA Ops:
  9.7 42.6 %reduce-scatter.2.cloned.1.call-done = bf16[1,256,1536]{2,1,0:T(8,128)(2,1)} async-done(((bf16[1,1024,1536]{2,1,0:T(8,128)(2,1)}), bf16[1,256,1536]{2,1,0:T(8,128)(2,1)}) %reduce-scatter.2.cloned.1.call-update) | async-done | bytes 786448 | tf_op jit(solution)/shard_map/reduce_scatter | solution.py:27
  52.3 2.1 fusion.6
  54.5 39.5 %psum.21 = f32[]{:T(128)} all-reduce(f32[]{:T(128)} %fusion.6), channel_id=1, replica_groups=mesh['expert'=2,'dp'=4,'shard'=4] {'expert','dp','shard'}, use_global_device_ids=true, to_apply=%region_2.0 | all-reduce | flops 1 | bytes 8 | tf_op jit(solution)/shard_map/psum | solution.py:35
  94.7 2.9 fusion.9
  97.6 1.6 convolution_bitcast_fusion.1
  99.5 92.3 %all-reduce.4.cloned.1.call-done = f32[1,384,384]{1,2,0:T(8,128)} async-done(((f32[1,384,384]{1,2,0:T(8,128)}), f32[1,384,384]{1,2,0:T(8,128)}) %all-reduce.4.cloned.1.call-update) | async-done | bytes 589840 | tf_op jit(solution)/shard_map/psum | solution.py:14
  194.1 11.7 %custom-call.26 = f32[1,128,128]{2,1,0:T(8,128)S(1)} custom-call(f32[1,128,128]{2,1,0:T(8,128)S(1)} %cholesky.192), custom_call_target="Cholesky" | custom-call | tf_op jit(solution)/shard_map/jit(cholesky)/cholesky | solution.py:17
  205.9 9.8 %custom-call.27 = f32[1,1,128,128]{2,3,1,0:T(8,128)S(1)} custom-call(f32[1,1,128,128]{3,2,1,0:T(8,128)S(1)} %get-tuple-element.33), custom_call_target="InvertDiagBlocksLowerTriangular" | custom-call | tf_op jit(solution)/shard_map/jit(cholesky)/cholesky | solution.py:17
  218.1 11.7 %custom-call.28 = f32[1,128,128]{2,1,0:T(8,128)S(1)} custom-call(f32[1,128,128]{2,1,0:T(8,128)S(1)} %cholesky.196), custom_call_target="Cholesky" | custom-call | tf_op jit(solution)/shard_map/jit(cholesky)/cholesky | solution.py:17
  229.9 10.0 %custom-call.29 = f32[1,1,128,128]{2,3,1,0:T(8,128)S(1)} custom-call(f32[1,1,128,128]{3,2,1,0:T(8,128)S(1)} %get-tuple-element.30), custom_call_target="InvertDiagBlocksLowerTriangular" | custom-call | tf_op jit(solution)/shard_map/jit(cholesky)/cholesky | solution.py:17
  241.2 11.7 %custom-call.30 = f32[1,128,128]{2,1,0:T(8,128)S(1)} custom-call(f32[1,128,128]{2,1,0:T(8,128)S(1)} %fusion.18), custom_call_target="Cholesky" | custom-call | tf_op jit(solution)/shard_map/jit(cholesky)/cholesky | solution.py:17
  257.2 9.0 %while.1 = (s32[]{:T(128)}, f32[1,384,384]{2,1,0:T(8,128)}, s32[3,2]{0,1:T(2,128)S(1)}, f32[3,1,128,128]{3,2,1,0:T(8,128)S(1)}, s32[]{:T(128)}) while((s32[]{:T(128)}, f32[1,384,384]{2,1,0:T(8,128)}, s32[3,2]{0,1:T(2,128)S(1)}, f32[3,1,128,128]{3,2,1,0:T(8,128)S(1)}, s32[]{:T(128)}) %tuple.31), condition=%wide.while_cond, body=%wide.while_body.sunk | while | flops 2 | bytes 131189 | solution.py:20
  257.8 2.3 bitcast_dynamic-update-slice_fusion.2
  260.9 2.3 bitcast_dynamic-update-slice_fusion.2
  263.9 2.3 bitcast_dynamic-update-slice_fusion.2
  266.2 29.5 %custom-call.31 = f32[1,3,128,128]{2,3,1,0:T(8,128)S(1)} custom-call(f32[1,3,128,128]{3,2,1,0:T(8,128)S(1)} %bitcast.165), custom_call_target="InvertDiagBlocksLowerTriangular" | custom-call | tf_op jit(solution)/shard_map/vmap(jit(_solve_triangular))/triangular_solve | solution.py:20
  299.4 3.5 convolution_bitcast_fusion
  303.2 97.9 %all-reduce.6.cloned.1.call-done = f32[1536,1,384]{0,2,1:T(8,128)} async-done(((f32[1536,1,384]{0,2,1:T(8,128)}), f32[1536,1,384]{0,2,1:T(8,128)}) %all-reduce.6.cloned.1.call-update) | async-done | bytes 2359312 | tf_op jit(solution)/shard_map/psum | solution.py:49
  401.1 2.0 multiply_reduce_fusion
  403.5 3.7 fusion.3
  408.1 1.7 copy.16
  409.8 5.3 %fusion.2 = f32[1,1,256,1536]{3,2,1,0:T(8,128)} fusion(f32[1536,1,384]{0,2,1:T(8,128)S(1)} %copy-done, bf16[1,256,1536]{2,1,0:T(8,128)(2,1)S(1)} %copy-done.2, f32[]{:T(128)S(6)} %div.15, f32[1,1,256,1536]{3,2,1,0:T(8,128)} %param.4, f32[1,128,256]{2,1,0:T(8,128)S(1)} %convolution_bitcast_fusion.3, f32[1,128,256]{2,1,0:T(8,128)S(1)} %convolution_bitcast_fusion.4, ...), kind=kOutput, calls=%fused_computation.7 | convolution fusion | flops 1814102016 | bytes 6684676 | tf_op jit(solution)/shard_map/emr,fer->emf/dot_general | solution.py:55
  415.1 19.6 %all-gather.6.cloned.1.call-done = bf16[1024,1536]{1,0:T(8,128)(2,1)} async-done(((bf16[256,1536]{1,0:T(8,128)(2,1)}), bf16[1024,1536]{1,0:T(8,128)(2,1)}) %all-gather.6.cloned.1.call-update) | async-done | bytes 3145744 | tf_op jit(solution)/shard_map/all_gather | solution.py:62
  434.7 3.8 copy.36
  (55 shorter events, 17.4 us)
Async XLA Ops:
  8.0 44.3 %reduce-scatter.2.cloned.1.call-start = ((), (), s32[]{:S(2)}) async-start(), calls=%async_computation.1 | async-start | bytes 3932160 | tf_op jit(solution)/shard_map/reduce_scatter | solution.py:27
  8.0 0.9 copy-start.5
  8.1 86.6 %copy-start.1 = (f32[1,1,256,1536]{3,2,1,0:T(8,128)S(1)}, f32[1,1,256,1536]{3,2,1,0:T(8,128)}, u32[]{:S(2)}) copy-start(f32[1,1,256,1536]{3,2,1,0:T(8,128)} %param.4) | copy-start | bytes 4718596
  8.7 85.9 %all-gather.4.cloned.1.call-start = ((), (), s32[]{:S(2)}) async-start(), calls=%async_computation.2 | async-start | bytes 1253376 | tf_op jit(solution)/shard_map/all_gather | solution.py:42
  9.6 182.2 %all-reduce.4.cloned.1.call-start = ((), (), s32[]{:S(2)}) async-start(), calls=%async_computation.3 | async-start | bytes 1179648 | tf_op jit(solution)/shard_map/psum | solution.py:14
  99.3 301.9 %all-reduce.6.cloned.1.call-start = ((), (), s32[]{:S(2)}) async-start(), calls=%async_computation.4 | async-start | bytes 4718592 | tf_op jit(solution)/shard_map/psum | solution.py:49
  191.8 1.4 copy-start.3
  193.3 0.8 copy-start.4
  257.1 42.2 %copy-start.2 = (bf16[1,256,1536]{2,1,0:T(8,128)(2,1)S(1)}, bf16[1,256,1536]{2,1,0:T(8,128)(2,1)}, u32[]{:S(2)}) copy-start(bf16[1,256,1536]{2,1,0:T(8,128)(2,1)} %reduce-scatter.2.cloned.1.call-done) | copy-start | bytes 2359300
  302.9 131.8 %all-gather.6.cloned.1.call-start = ((), (), s32[]{:S(2)}) async-start(), calls=%async_computation.5 | async-start | bytes 3932160 | tf_op jit(solution)/shard_map/all_gather | solution.py:62
  401.1 2.4 copy-start
Sparse Core Ops, SparseCore 0:
  11.3 40.9 reduce-scatter.1
  407.3 27.3 all-gather.5
Sparse Core Ops, SparseCore 1:
  12.1 50.7 all-gather.3
  99.3 92.4 all-reduce.3
  303.0 98.1 all-reduce.5
where the time goes:
time: 447 us; the launch traced here: 446 us
  waiting for transfers between devices  253 us (57%)
  other arithmetic  91.9 us (21%)
  blocking collectives  39.5 us (9%)
  matrix products  24.4 us (5%)
  between operations  18.6 us (4%)
  local copies, waits for them, and re-layouts  17.8 us (4%)
    psum x1, waiting for transfers between devices, shards(): right_factor = lax.psum(right_term, ('dp', 'shard'))  97.9 us
    psum x1, waiting for transfers between devices, orthonormal(): lax.psum(jnp.einsum('emr,ems->ers', projected, projected, precision=highe...  92.3 us
    another operation x10, other arithmetic, orthonormal(): triangles = jnp.linalg.cholesky(gram_matrix)  56.4 us
    reduce_scatter x1, waiting for transfers between devices, shards(): lax.psum_scatter(partial_value, 'dp', scatter_dimension=1, tiled=True)  42.6 us
    psum x1, blocking collectives, shards(): lax.psum(jnp.sum(gradient * gradient), ('expert', 'dp', 'shard'))  39.5 us
    another operation x3, other arithmetic, solve_one(): return jax.scipy.linalg.solve_triangular(triangle, columns.T, lower=True).T  30.4 us
    all_gather x1, waiting for transfers between devices, shards(): weight_update = lax.all_gather(local_update, 'dp', axis=1, tiled=True)  19.6 us
    another operation x9, local copies, waits for them, and re-layouts  8.96 us
  transfers between devices with their start and end apart: 5, of which 4 were waited for; matrix products, arithmetic and copies ran while one was open for 2% of the time, Pallas kernels for 0%

commit v1 on v0

v1 whole, which is shorter than its diff:
```python
import functools
import math

import jax
import jax.numpy as jnp
from jax import lax
from jax.experimental import pallas as pl
from jax.experimental.pallas import tpu as pltpu
from jax.sharding import PartitionSpec as P

clip_rms = 0.5
keep_share = 0.95
highest = lax.Precision.HIGHEST
f32 = jnp.float32
bf16 = jnp.bfloat16


def split(a):
    hi = a.astype(bf16)
    return hi, (a - hi.astype(f32)).astype(bf16)


def contract(a, b, da, db):
    return lax.dot_general(a, b, (((da,), (db,)), ((), ())), preferred_element_type=f32)


def exact(a, b, da, db):
    return lax.dot_general(
        a, b, (((da,), (db,)), ((), ())), precision=highest, preferred_element_type=f32
    )


def inverse_factor(block):
    width = block.shape[0]
    panels = width // 8
    sub = lax.broadcasted_iota(jnp.int32, (8, width), 0)
    lane = lax.broadcasted_iota(jnp.int32, (8, width), 1)
    a = [block[8 * p : 8 * p + 8, :] for p in range(panels)]
    x = [jnp.where(lane == sub + 8 * p, 1.0, 0.0).astype(f32) for p in range(panels)]
    for j in range(width):
        p, r = divmod(j, 8)
        arow = a[p][r : r + 1, :]
        xrow = x[p][r : r + 1, :]
        scale = 1.0 / arow[:, j : j + 1]
        arow = arow * scale
        xrow = xrow * scale
        for q in range(p if r < 7 else p + 1, panels):
            col = a[q][:, j : j + 1]
            if q == p:
                col = jnp.where(sub[:, :1] > r, col, 0.0)
            a[q] = a[q] - col * arow
            x[q] = x[q] - col * xrow
        if r == 7:
            diag = jnp.sum(jnp.where(lane == sub + 8 * p, a[p], 0.0), axis=1, keepdims=True)
            x[p] = x[p] * lax.rsqrt(diag)
    return jnp.concatenate(x, axis=0)


def inverse_triangle(gram_ref, w_ref):
    rank = gram_ref.shape[0]
    size = 128 if rank % 128 == 0 else rank
    count = rank // size
    s = {
        (i, k): gram_ref[i * size : (i + 1) * size, k * size : (k + 1) * size]
        for i in range(count)
        for k in range(i + 1)
    }
    low = {}
    w = {}
    w_ref[...] = jnp.zeros_like(w_ref)
    for k in range(count):
        w[k, k] = inverse_factor(s[k, k])
        for i in range(k + 1, count):
            low[i, k] = exact(s[i, k], w[k, k], 1, 1)
        for i in range(k + 1, count):
            for m in range(k + 1, i + 1):
                s[i, m] = s[i, m] - exact(low[i, k], low[m, k], 1, 1)
        for m in range(k):
            total = exact(low[k, m], w[m, m], 1, 0)
            for t in range(m + 1, k):
                total = total + exact(low[k, t], w[t, m], 1, 0)
            w[k, m] = -exact(w[k, k], total, 1, 0)
        for m in range(k + 1):
            w_ref[k * size : (k + 1) * size, m * size : (m + 1) * size] = w[k, m]


def finish_kernel(unit_scale, q_ref, m_ref, rows_ref, buf_ref, mine_ref, nm_ref, right_ref, inv_ref, wu_ref, gram, w):
    qv = q_ref[...]
    m_hi, m_lo = split(m_ref[...])
    gram[...] = contract(qv, m_hi, 0, 0) + contract(qv, m_lo, 0, 0)
    inverse_triangle(gram, w)
    w_hi, w_lo = split(w[...])
    right = contract(m_hi, w_hi, 1, 1) + contract(m_hi, w_lo, 1, 1) + contract(m_lo, w_hi, 1, 1)
    right_ref[...] = right
    inverse = lax.rsqrt(jnp.sum(right * right, axis=0, keepdims=True) + 1e-06)
    inv_ref[...] = inverse
    right_b = right.astype(bf16)
    mine_hi, mine_lo = split(mine_ref[...])
    basis = contract(mine_hi, w_hi, 1, 1) + contract(mine_hi, w_lo, 1, 1) + contract(mine_lo, w_hi, 1, 1)
    nm_ref[...] = buf_ref[...] - (1.0 - keep_share) * contract(basis.astype(bf16), right_b, 1, 1)
    rows = rows_ref[...]
    every = contract(rows, w_hi, 1, 1) + contract(rows, w_lo, 1, 1)
    scaled = (every * (unit_scale * inverse)).astype(bf16)
    wu_ref[...] = contract(scaled, right_b, 1, 1).astype(bf16)


def finish(unit_scale, q, m, rows, buf, mine):
    hidden, rank = m.shape
    whole = pl.BlockSpec(memory_space=pltpu.VMEM)
    return pl.pallas_call(
        functools.partial(finish_kernel, unit_scale),
        out_shape=(
            jax.ShapeDtypeStruct(buf.shape, f32),
            jax.ShapeDtypeStruct((hidden, rank), f32),
            jax.ShapeDtypeStruct((1, rank), f32),
            jax.ShapeDtypeStruct((rows.shape[0], hidden), bf16),
        ),
        in_specs=[whole] * 5,
        out_specs=(whole,) * 4,
        scratch_shapes=[pltpu.VMEM((rank, rank), f32), pltpu.VMEM((rank, rank), f32)],
        compiler_params=pltpu.CompilerParams(vmem_limit_bytes=56 * 1024 * 1024),
    )(q, m, rows, buf, mine)


def shards(grad_partials, momentum, q_factor):
    partial_value = grad_partials[0]
    gradient = lax.psum_scatter(partial_value, "dp", scatter_dimension=1, tiled=True).astype(f32)
    momentum_rows = momentum[:, 0]
    experts, local_rows, hidden_width = gradient.shape
    factor_count, _, rank_width = q_factor.shape
    total_rows = local_rows * lax.axis_size("dp") * lax.axis_size("shard")
    entries = float(experts * lax.axis_size("expert") * total_rows * hidden_width)
    square_sum = lax.psum(jnp.sum(gradient * gradient), ("expert", "dp", "shard"))
    clip_scale = clip_rms / jnp.sqrt(square_sum / entries + 1e-06)
    buffer = (momentum_rows + clip_scale * gradient)[0]
    q_all = lax.all_gather(q_factor.astype(bf16)[:, 0], ("dp", "shard"), axis=0, tiled=True)
    projected = exact(buffer, q_all.astype(f32), 1, 0)
    moment = lax.psum(exact(buffer, projected, 0, 0), ("dp", "shard"))
    rows = lax.all_gather(projected.astype(bf16), "dp", axis=0, tiled=True)
    unit_scale = math.sqrt(total_rows * hidden_width / rank_width)
    next_momentum, right, inverse, update = finish(unit_scale, q_all, moment, rows, buffer, projected)
    offset = (
        lax.axis_index("dp") * lax.axis_size("shard") + lax.axis_index("shard")
    ) * factor_count
    next_factor = lax.dynamic_slice_in_dim(right, offset, factor_count, 0) * inverse
    return (next_momentum[None, None], next_factor[:, None], update[None])


def solution(mesh):
    placed = (
        P("dp", "expert", "shard", None),
        P("expert", "shard", "dp", None),
        P(("dp", "shard"), "expert", None),
    )
    return jax.shard_map(
        shards,
        mesh=mesh,
        in_specs=placed,
        out_specs=(
            P("expert", "shard", "dp", None),
            P(("dp", "shard"), "expert", None),
            P("expert", "shard", None),
        ),
        check_vma=False,
    )
```

time: 447 us -> 259 us (0.58)
  waiting for transfers between devices: 253 us -> 133 us
  other arithmetic: 91.9 us -> 5.1 us
  Pallas kernels: 0 us -> 45.4 us
  matrix products: 24.4 us -> 7.27 us
  local copies, waits for them, and re-layouts: 17.8 us -> 1.64 us
  blocking collectives: 39.5 us -> 49.7 us
    psum x2 -> x1, waiting for transfers between devices: 190 us -> 89.8 us  [shards(): moment = lax.psum(exact(buffer, projected, 0, 0), ('dp', 'shard'))]
    another operation x13 -> x0, other arithmetic: 86.8 us -> none  [the longest x10 56.4 us: orthonormal(): triangles = jnp.linalg.cholesky(gram_matrix)]
    pallas_call x0 -> x1, Pallas kernels: none -> 45.4 us  [finish(): pl.pallas_call(functools.partial(finish_kernel, unit_scale), out_shape=(j...]
    all_gather x2 -> x1, waiting for transfers between devices: 19.6 us -> 0.03 us  [shards(): lax.all_gather(q_factor.astype(bf16)[:, 0], ('dp', 'shard'), axis=0, tile...]
    all_gather x0 -> x1, blocking collectives: none -> 10.2 us  [shards(): rows = lax.all_gather(projected.astype(bf16), 'dp', axis=0, tiled=True)]
    dot_general x5 -> x2, matrix products: 17.1 us -> 7.27 us  [exact(): lax.dot_general(a, b, (((da,), (db,)), ((), ())), precision=highest, pref...]
    another operation x13 -> x0, local copies, waits for them, and re-layouts: 9.01 us -> none
    another operation x9 -> x0, matrix products: 7.33 us -> none  [the longest x4 3.67 us: orthonormal(): triangles = jnp.linalg.cholesky(gram_matrix)]
  transfers between devices with their start and end apart: 5 -> 3, of which waited for: 4 -> 2; matrix products, arithmetic and copies ran while one was open for 2% -> 2% of each run, Pallas kernels for 0% -> 0%
where the time goes in v1:
time: 259 us
  waiting for transfers between devices  133 us (51%)
  blocking collectives  49.7 us (19%)
  Pallas kernels  45.4 us (18%)
  between operations  16.3 us (6%)
  matrix products  7.27 us (3%)
  other arithmetic  5.1 us (2%)
    psum x1, waiting for transfers between devices, shards(): moment = lax.psum(exact(buffer, projected, 0, 0), ('dp', 'shard'))  89.8 us
    pallas_call x1, Pallas kernels, finish(): pl.pallas_call(functools.partial(finish_kernel, unit_scale), out_shape=(j...  45.4 us
    reduce_scatter x1, waiting for transfers between devices, shards(): lax.psum_scatter(partial_value, 'dp', scatter_dimension=1, tiled=True)  42.6 us
    psum x1, blocking collectives, shards(): lax.psum(jnp.sum(gradient * gradient), ('expert', 'dp', 'shard'))  39.5 us
    all_gather x1, blocking collectives, shards(): rows = lax.all_gather(projected.astype(bf16), 'dp', axis=0, tiled=True)  10.2 us
    dot_general x2, matrix products, exact(): lax.dot_general(a, b, (((da,), (db,)), ((), ())), precision=highest, pref...  7.27 us
  transfers between devices with their start and end apart: 3, of which 2 were waited for; matrix products, arithmetic and copies ran while one was open for 2% of the time, Pallas kernels for 0%

profile of v1, /device:TPU:0, one launch (start us, length us, event | category | flops | bytes accessed | tf_op | source)
XLA Modules:
  0.0 258.7 jit_solution(17605962057040300426)
XLA Ops:
  8.0 0.0 reduce-scatter.2.cloned.1.call-start
  8.0 0.0 copy-start.3
  8.1 0.7 reduce-scatter.2.cloned.1.call-update
  8.7 0.0 all-gather.3.cloned.1.call-start
  8.8 0.2 copy-done.3
  9.0 0.6 copy.9
  9.6 0.0 all-gather.3.cloned.1.call-update
  9.6 0.0 all-reduce.2.cloned.1.call-start
  9.7 42.6 %reduce-scatter.2.cloned.1.call-done = bf16[1,256,1536]{2,1,0:T(8,128)(2,1)} async-done(((bf16[1,1024,1536]{2,1,0:T(8,128)(2,1)}), bf16[1,256,1536]{2,1,0:T(8,128)(2,1)}) %reduce-scatter.2.cloned.1.call-update) | async-done | bytes 786448 | tf_op jit(solution)/shard_map/reduce_scatter | solution.py:127
  52.3 2.1 fusion
  54.5 39.5 %psum.14 = f32[]{:T(128)} all-reduce(f32[]{:T(128)} %fusion), channel_id=1, replica_groups=mesh['expert'=2,'dp'=4,'shard'=4] {'expert','dp','shard'}, use_global_device_ids=true, to_apply=%region_2.0 | all-reduce | flops 1 | bytes 8 | tf_op jit(solution)/shard_map/psum | solution.py:133
  94.6 0.0 copy-done.2
  94.7 1.3 fusion.2.buf_ref
  96.0 0.0 copy-start
  96.0 0.0 all-gather.3.cloned.1.call-done
  96.0 3.2 %fusion.5 = (bf16[256,384]{1,0:T(8,128)(2,1)S(1)}, f32[256,384]{1,0:T(8,128)S(1)}) fusion(f32[256,1536]{1,0:T(8,128)S(1)} %fusion.2.buf_ref, bf16[1536,1,384]{2,0,1:T(8,128)(2,1)} %all-gather.3.cloned.1.call-done), kind=kOutput, calls=%fused_computation.9 | convolution fusion | flops 1812037632 | bytes 3342336 | tf_op jit(solution)/shard_map/dot_general | solution.py:28
  99.3 4.1 %fusion.6 = f32[1536,384]{1,0:T(8,128)} fusion(f32[256,1536]{1,0:T(8,128)S(1)} %fusion.2.buf_ref, f32[256,384]{1,0:T(8,128)S(1)} %get-tuple-element.15.mine_ref), kind=kOutput, calls=%fused_computation.10 | convolution fusion | flops 1811939328 | bytes 4325376 | tf_op jit(solution)/shard_map/dot_general | solution.py:28
  103.3 0.0 all-reduce.2.cloned.1.call-update
  103.4 10.2 %all_gather.7.rows_ref = bf16[1024,384]{1,0:T(8,128)(2,1)} all-gather(bf16[256,384]{1,0:T(8,128)(2,1)S(1)} %get-tuple-element.14), channel_id=1, replica_groups=mesh['expert'=2,'dp'=4,'shard'=4] {'dp'}, dimensions={0}, use_global_device_ids=true | all-gather | bytes 983040 | tf_op jit(solution)/shard_map/all_gather | solution.py:139
  113.6 89.8 %all-reduce.2.cloned.1.call-done.m_ref = f32[1536,384]{1,0:T(8,128)} async-done(((f32[1536,384]{1,0:T(8,128)}), f32[1536,384]{1,0:T(8,128)}) %all-reduce.2.cloned.1.call-update) | async-done | bytes 2359312 | tf_op jit(solution)/shard_map/psum | solution.py:138
  203.4 45.4 %shard_map.58 = (f32[256,1536]{1,0:T(8,128)}, f32[1536,384]{1,0:T(8,128)}, f32[1,384]{1,0:T(1,128)}, bf16[1024,1536]{1,0:T(8,128)(2,1)}) custom-call(bf16[1536,384]{1,0:T(8,128)(2,1)} %bitcast.17, f32[1536,384]{1,0:T(8,128)} %all-reduce.2.cloned.1.call-done.m_ref, bf16[1024,384]{1,0:T(8,128)(2,1)} %all_gather.7.rows_ref, f32[256,1536]{1,0:T(8,128)} %copy-done, ...), custom_call_target="tpu_custom_call" | custom-call | tf_op jit(solution)/shard_map/pallas_call | solution.py:110
  248.8 0.7 reduce
  249.5 0.9 multiply_bitcast_fusion
  250.4 0.8 copy.7
  (4 shorter events, 0.0 us)
Async XLA Ops:
  8.0 44.3 %reduce-scatter.2.cloned.1.call-start = ((), (), s32[]{:S(2)}) async-start(), calls=%async_computation.1 | async-start | bytes 3932160 | tf_op jit(solution)/shard_map/reduce_scatter | solution.py:127
  8.0 0.9 copy-start.3
  8.1 86.6 %copy-start.2 = (f32[1,1,256,1536]{3,2,1,0:T(8,128)S(1)}, f32[1,1,256,1536]{3,2,1,0:T(8,128)}, u32[]{:S(2)}) copy-start(f32[1,1,256,1536]{3,2,1,0:T(8,128)} %param.4) | copy-start | bytes 4718596
  8.7 87.3 %all-gather.3.cloned.1.call-start = ((), (), s32[]{:S(2)}) async-start(), calls=%async_computation.3 | async-start | bytes 1253376 | tf_op jit(solution)/shard_map/all_gather | solution.py:136
  9.6 193.8 %all-reduce.2.cloned.1.call-start = ((), (), s32[]{:S(2)}) async-start(), calls=%async_computation.2 | async-start | bytes 4718592 | tf_op jit(solution)/shard_map/psum | solution.py:138
  96.0 3.3 %copy-start = (f32[256,1536]{1,0:T(8,128)}, f32[256,1536]{1,0:T(8,128)S(1)}, u32[]{:S(2)}) copy-start(f32[256,1536]{1,0:T(8,128)S(1)} %fusion.2.buf_ref) | copy-start | bytes 4718596
  99.3 4.1 %copy-start.1 = (f32[256,384]{1,0:T(8,128)}, f32[256,384]{1,0:T(8,128)S(1)}, u32[]{:S(2)}) copy-start(f32[256,384]{1,0:T(8,128)S(1)} %get-tuple-element.15.mine_ref) | copy-start | bytes 1179652
Sparse Core Ops, SparseCore 0:
  11.3 40.9 reduce-scatter.1
Sparse Core Ops, SparseCore 1:
  12.1 50.7 all-gather.2
  103.5 99.9 all-reduce.1
